TPU v7x, 32 devices: a whole 2x2x4 slice. The times are simulated.
32 devices in a mesh: dp: 8 (over y, x, core), expert: 4 (over z).
Axes of the slice: x: 2, y: 2, z: 4, core: 2. Of those that a mesh axis runs over, the one named last changes fastest.
Arguments:
- tokens: bfloat16 [4096, 2048], P(('dp', 'expert')), may hold values from -6 to 6
- cotangent: bfloat16 [4096, 2048], P(('dp', 'expert')), may hold values from -6 to 6
- expert_ids: int32 [4096, 2], P(('dp', 'expert')), may hold values from 0 to 3, all different within a row; in each aligned block of 128 rows (0 to 127, 128 to 255, ...) at most 128 rows name the same one
- combine: float32 [4096, 2], P(('dp', 'expert')), may hold values from 0.1 to 1
- w_gate: bfloat16 [4, 2048, 768], P('expert'), may hold values from -0.125 to 0.125
- w_up: bfloat16 [4, 2048, 768], P('expert'), may hold values from -0.125 to 0.125
- w_down: bfloat16 [4, 768, 2048], P('expert'), may hold values from -0.21875 to 0.21875
Outputs:
- input_grad: bfloat16 [4096, 2048], P(('dp', 'expert'))
- combine_grad: float32 [4096, 2], P(('dp', 'expert'))
- gate_grad: bfloat16 [4, 2048, 768], P('expert', 'dp')
- up_grad: bfloat16 [4, 2048, 768], P('expert', 'dp')
- down_grad: bfloat16 [4, 768, 2048], P('expert', 'dp')
Inputs may be any that keep to these rules, and one draw needn't show every extreme that they name: `expert_ids`: each token names 2 different experts. In the rows of one device no expert is named by more than 128 tokens, and in some devices' rows some expert is named by exactly 128.
All inputs are finite; a program needn't handle non-finite values.
Results may differ from a plain program's by a relative error of at most 0.02.
Values may be sent and summed in bfloat16 or wider, within the bound.
A program may use at most 128 MiB of HBM per device.

v0:
```python
import jax
import jax.numpy as jnp
from jax import lax
from jax.sharding import PartitionSpec as P


def slot_table(expert_ids, experts_all, capacity):
    pairs = expert_ids.reshape(-1)
    count = pairs.shape[0]
    onehot = (pairs[:, None] == jnp.arange(experts_all, dtype=jnp.int32)[None, :]).astype(jnp.int32)
    before = jnp.cumsum(onehot, axis=0) - onehot
    position = jnp.sum(before * onehot, axis=1)
    dest = pairs * capacity + position
    filled = (
        jnp.zeros((experts_all * capacity,), jnp.int32)
        .at[dest]
        .set(jnp.arange(count, dtype=jnp.int32) + 1)
    )
    return (dest, filled)


def gather_rows(tokens, cotangent, combine, filled, top):
    live = filled > 0
    pair = jnp.maximum(filled - 1, 0)
    source = pair // top
    rows_x = jnp.where(live[:, None], jnp.take(tokens, source, axis=0), jnp.zeros((), tokens.dtype))
    rows_dy = jnp.where(
        live[:, None], jnp.take(cotangent, source, axis=0), jnp.zeros((), cotangent.dtype)
    )
    rows_c = jnp.where(
        live, jnp.take(combine.reshape(-1), pair, axis=0), jnp.zeros((), combine.dtype)
    )
    return (rows_x, rows_dy, rows_c)


def forward_part(rows_x, gate_mat, up_mat, down_mat):
    gate = jnp.dot(rows_x, gate_mat, preferred_element_type=jnp.float32)
    up = jnp.dot(rows_x, up_mat, preferred_element_type=jnp.float32)
    sig = jax.nn.sigmoid(gate)
    act = gate * sig
    hidden = (act * up).astype(jnp.bfloat16)
    output = jnp.dot(hidden, down_mat, preferred_element_type=jnp.float32)
    return (gate, up, sig, act, hidden, output)


def backward_part(state, rows_dy, rows_c, gate_mat, up_mat, down_mat):
    gate, up, sig, act, hidden, output = state
    comb_grad = jnp.sum(rows_dy.astype(jnp.float32) * output, axis=1)
    scaled = (rows_c[:, None] * rows_dy.astype(jnp.float32)).astype(jnp.bfloat16)
    last = (((1,), (1,)), ((), ()))
    hidden_grad = lax.dot_general(scaled, down_mat, last, preferred_element_type=jnp.float32)
    gate_d = (hidden_grad * up * (sig * (1.0 + gate * (1.0 - sig)))).astype(jnp.bfloat16)
    up_d = (hidden_grad * act).astype(jnp.bfloat16)
    row_grad = lax.dot_general(gate_d, gate_mat, last, preferred_element_type=jnp.float32)
    row_grad = (
        row_grad + lax.dot_general(up_d, up_mat, last, preferred_element_type=jnp.float32)
    ).astype(jnp.bfloat16)
    return (comb_grad, scaled, gate_d, up_d, row_grad)


def shards(tokens, cotangent, expert_ids, combine, w_gate, w_up, w_down):
    first = (((0,), (0,)), ((), ()))
    local_experts = w_gate.shape[0]
    groups = lax.axis_size("expert")
    replicas = lax.axis_size("dp")
    experts_all = local_experts * groups
    tok_rows, top = expert_ids.shape
    feature = tokens.shape[1]
    hidden_width = w_gate.shape[2]
    capacity = 2 * tok_rows * top // experts_all
    dest, filled = slot_table(expert_ids, experts_all, capacity)
    rows_x, rows_dy, rows_c = gather_rows(tokens, cotangent, combine, filled, top)
    rows_x = rows_x.reshape(experts_all, capacity, feature)
    rows_dy = rows_dy.reshape(experts_all, capacity, feature)
    rows_c = rows_c.reshape(experts_all, capacity)
    recv_x, recv_dy, recv_c = (
        lax.all_to_all(rows_x, "expert", split_axis=0, concat_axis=1, tiled=True),
        lax.all_to_all(rows_dy, "expert", split_axis=0, concat_axis=1, tiled=True),
        lax.all_to_all(
            rows_c.astype(jnp.bfloat16), "expert", split_axis=0, concat_axis=1, tiled=True
        ).astype(rows_c.dtype),
    )
    states = forward_part(recv_x[0], w_gate[0], w_up[0], w_down[0])
    comb_grad, scaled, gate_d, up_d, row_grad = backward_part(
        states, recv_dy[0], recv_c[0], w_gate[0], w_up[0], w_down[0]
    )
    row_list = [row_grad]
    comb_list = [comb_grad]
    inputs = recv_x[0]
    hidden = states[4]
    paired = jnp.concatenate([gate_d, up_d], axis=1)

    def gate_up_term(start, count, inputs=inputs, paired=paired):
        return lax.dot_general(inputs, paired, first, preferred_element_type=jnp.float32)

    def down_term(start, count, hidden=hidden, scaled=scaled):
        return lax.dot_general(hidden, scaled, first, preferred_element_type=jnp.float32)

    both = lax.psum_scatter(
        gate_up_term(jnp.int32(0), feature // replicas * lax.axis_size("dp")).astype(jnp.bfloat16),
        "dp",
        scatter_dimension=0,
        tiled=True,
    ).astype(jnp.float32)
    gate_terms = [both[:, :hidden_width].astype(jnp.bfloat16)]
    up_terms = [both[:, hidden_width:].astype(jnp.bfloat16)]
    down_sum = lax.psum_scatter(
        down_term(jnp.int32(0), hidden_width // replicas * lax.axis_size("dp")).astype(
            jnp.bfloat16
        ),
        "dp",
        scatter_dimension=0,
        tiled=True,
    )
    down_terms = [down_sum]
    gate_grad = jnp.stack(gate_terms)
    up_grad = jnp.stack(up_terms)
    down_grad = jnp.stack(down_terms)
    back_rows, back_comb = (
        lax.all_to_all(jnp.stack(row_list), "expert", split_axis=1, concat_axis=0, tiled=True),
        lax.all_to_all(
            jnp.stack(comb_list).astype(jnp.bfloat16),
            "expert",
            split_axis=1,
            concat_axis=0,
            tiled=True,
        ).astype(jnp.float32),
    )
    flat_rows = back_rows.reshape(experts_all * capacity, feature)
    picked = jnp.take(flat_rows, dest, axis=0).reshape(tok_rows, top, feature)
    input_grad = jnp.sum(picked.astype(jnp.float32), axis=1).astype(jnp.bfloat16)
    combine_grad = jnp.take(back_comb.reshape(-1), dest, axis=0).reshape(tok_rows, top)
    return (input_grad, combine_grad, gate_grad, up_grad, down_grad)


def solution(mesh):
    placed = (
        P(("dp", "expert"), None),
        P(("dp", "expert"), None),
        P(("dp", "expert"), None),
        P(("dp", "expert"), None),
        P("expert", None, None),
        P("expert", None, None),
        P("expert", None, None),
    )
    return jax.shard_map(
        shards,
        mesh=mesh,
        in_specs=placed,
        out_specs=(
            P(("dp", "expert"), None),
            P(("dp", "expert"), None),
            P("expert", "dp", None),
            P("expert", "dp", None),
            P("expert", "dp", None),
        ),
        check_vma=False,
    )
```

profile of v0, /device:TPU:0, one launch (start us, length us, event | category | flops | bytes accessed | tf_op | source)
XLA Modules:
  0.0 287.7 jit_solution(16933779392859275133)
XLA Ops:
  12.6 3.4 %gather_fusion = bf16[512]{0:T(512)(128)(2,1)S(1)} fusion(bf16[256]{0:T(256)(128)(2,1)S(1)} %reshape.180, s32[1024]{0:T(1024)S(1)} %pad_clamp_fusion.2), kind=kCustom, calls=%fused_computation.2 | custom fusion | bytes 4096 | tf_op jit(solution)/shard_map/jit(_take)/gather | solution.py:31
  16.6 6.3 %all-to-all-start = ((bf16[4,1,128]{2,1,0:T(2,128)(2,1)}), bf16[4,1,128]{2,1,0:T(2,128)(2,1)S(1)}, u32[]{:S(2)}, u32[]{:S(2)}) async-start(bf16[4,1,128]{2,1,0:T(2,128)(2,1)} %copy.36), calls=%async_computation | async-start | bytes 4096 | tf_op jit(solution)/shard_map/all_to_all | solution.py:79
  23.0 6.3 %gather_fusion.4 = bf16[512,2048]{1,0:T(8,128)(2,1)} fusion(bf16[128,2048]{1,0:T(8,128)(2,1)} %param.9, s32[1024]{0:T(1024)S(1)} %pad_clamp_fusion.1), kind=kCustom, calls=%fused_computation.1.clone | custom fusion | bytes 4196352 | tf_op jit(solution)/shard_map/jit(_take)/gather | solution.py:26
  29.3 6.4 %gather_fusion.3 = bf16[512,2048]{1,0:T(8,128)(2,1)} fusion(bf16[128,2048]{1,0:T(8,128)(2,1)} %param.10, s32[1024]{0:T(1024)S(1)} %pad_clamp_fusion.1), kind=kCustom, calls=%fused_computation.clone | custom fusion | bytes 4196352 | tf_op jit(solution)/shard_map/jit(_take)/gather | solution.py:28
  35.7 4.0 %select_select_fusion.1 = (bf16[512,2048]{1,0:T(8,128)(2,1)}, bf16[512,2048]{1,0:T(8,128)(2,1)}) fusion(bf16[512,2048]{1,0:T(8,128)(2,1)} %gather_fusion.3, pred[512]{0:T(512)(128)(4,1)S(1)} %get-tuple-element.25, pred[512]{0:T(512)(128)(4,1)S(1)} %get-tuple-element.24, bf16[512,2048]{1,0:T(8,128)(2,1)} %gather_fusion.4), kind=kLoop, calls=%fused_computation.29 | loop fusion | flops 4194304 | bytes 8389632 | tf_op jit(solution)/shard_map/jit(_where)/select_n | solution.py:27
  39.7 52.8 %all_to_all.22 = bf16[4,128,2048]{2,1,0:T(8,128)(2,1)} all-to-all(bf16[4,128,2048]{2,1,0:T(8,128)(2,1)} %bitcast.90), channel_id=1, replica_groups=mesh['dp'=8,'expert'=4] {'expert'}, dimensions={0} | all-to-all | bytes 4194304 | tf_op jit(solution)/shard_map/all_to_all | solution.py:77
  92.5 4.5 %all-to-all-start.1 = ((bf16[4,128,2048]{2,1,0:T(8,128)(2,1)}), bf16[4,128,2048]{2,1,0:T(8,128)(2,1)}, u32[]{:S(2)}, u32[]{:S(2)}) async-start(bf16[4,128,2048]{2,1,0:T(8,128)(2,1)} %bitcast.89), calls=%async_computation.1 | async-start | bytes 4194304 | tf_op jit(solution)/shard_map/all_to_all | solution.py:78
  97.2 5.5 %fusion.5 = f32[512,768]{1,0:T(8,128)} fusion(bf16[512,2048]{1,0:T(8,128)(2,1)} %bitcast.91, bf16[1,2048,768]{2,1,0:T(8,128)(2,1)} %param.13), kind=kOutput, calls=%fused_computation.17 | convolution fusion | flops 1610612736 | bytes 6815744 | tf_op jit(solution)/shard_map/dot_general | solution.py:37
  102.7 41.5 %all-to-all-done.1 = bf16[4,128,2048]{2,1,0:T(8,128)(2,1)} async-done(((bf16[4,128,2048]{2,1,0:T(8,128)(2,1)}), bf16[4,128,2048]{2,1,0:T(8,128)(2,1)}, u32[]{:S(2)}, u32[]{:S(2)}) %all-to-all-start.1) | async-done | bytes 2097184 | tf_op jit(solution)/shard_map/all_to_all | solution.py:78
  148.8 3.2 %multiply_convert_fusion = (bf16[512,768]{1,0:T(8,128)(2,1)}, bf16[512,768]{1,0:T(8,128)(2,1)S(1)}, bf16[512,768]{1,0:T(8,128)(2,1)S(1)}) fusion(f32[512,768]{1,0:T(8,128)S(1)} %copy-done.7, f32[512,768]{1,0:T(8,128)S(1)} %fusion.12, bf16[512,2048]{1,0:T(8,128)(2,1)S(1)} %bitcast.92, bf16[1,2048,768]{2,1,0:T(8,128)(2,1)S(1)} %copy-done), kind=kOutput, calls=%fused_computation.34 | convolution fusion | flops 1616510976 | bytes 10747904 | tf_op jit(solution)/shard_map/dot_general | solution.py:38
  153.1 5.5 %convolution_convert_fusion = bf16[2048,1536]{1,0:T(8,128)(2,1)} fusion(bf16[512,2048]{1,0:T(8,128)(2,1)S(1)} %bitcast.93, bf16[512,768]{1,0:T(8,128)(2,1)S(1)} %get-tuple-element.29, bf16[512,768]{1,0:T(8,128)(2,1)S(1)} %get-tuple-element.28), kind=kOutput, calls=%fused_computation.6 | convolution fusion | flops 3227516928 | bytes 9961472 | tf_op jit(solution)/shard_map/dot_general | solution.py:94
  158.7 4.7 %fusion.1 = bf16[512]{0:T(512)(128)(2,1)S(1)} fusion(bf16[4,128,2048]{2,1,0:T(8,128)(2,1)} %all-to-all-done.1, bf16[512,768]{1,0:T(8,128)(2,1)} %get-tuple-element.27, bf16[1,768,2048]{2,1,0:T(8,128)(2,1)} %param.15), kind=kOutput, calls=%fused_computation.11 | convolution fusion | flops 1613757952 | bytes 6030336 | tf_op jit(solution)/shard_map/dot_general | solution.py:42
  163.9 3.2 %all-to-all-start.4 = ((bf16[1,4,128]{2,0,1:T(2,128)(2,1)}), bf16[1,4,128]{2,0,1:T(2,128)(2,1)S(1)}, u32[]{:S(2)}, u32[]{:S(2)}) async-start(bf16[1,4,128]{2,0,1:T(2,128)(2,1)} %copy.38), calls=%async_computation.4 | async-start | bytes 4096 | tf_op jit(solution)/shard_map/all_to_all | solution.py:121
  169.8 3.6 %convolution_convert_fusion.1 = bf16[768,2048]{1,0:T(8,128)(2,1)} fusion(bf16[512,768]{1,0:T(8,128)(2,1)S(1)} %copy-done.6, bf16[512,2048]{1,0:T(8,128)(2,1)S(1)} %fusion.2), kind=kOutput, calls=%fused_computation.14 | convolution fusion | flops 1612185600 | bytes 6029312 | tf_op jit(solution)/shard_map/dot_general | solution.py:97
  173.5 4.1 %fusion.3 = f32[512,2048]{1,0:T(8,128)S(1)} fusion(bf16[512,768]{1,0:T(8,128)(2,1)} %copy-done.5, bf16[1,2048,768]{2,1,0:T(8,128)(2,1)} %param.13), kind=kOutput, calls=%fused_computation.15 | convolution fusion | flops 1610612736 | bytes 8126464 | tf_op jit(solution)/shard_map/dot_general | solution.py:54
  179.4 5.3 %copy.46 = bf16[1,512,2048]{2,0,1:T(2,128)(2,1)} copy(bf16[1,512,2048]{2,1,0:T(8,128)(2,1)S(1)} %fusion.16) | data formatting | bytes 4194304 | tf_op jit(solution)/shard_map/stack | solution.py:120
  185.1 14.5 %reduce.1 = bf16[512,2048]{1,0:T(8,128)(2,1)} reduce(bf16[512,1,2048]{2,1,0:T(2,128)(2,1)} %bitcast.87, bf16[]{:T(256)} %broadcast.139), dimensions={1}, to_apply=%bitcast.83.reduce_sub_computation | reduce | bytes 4194306
  199.6 4.6 %reshape.245 = bf16[4,2,131072]{2,1,0:T(2,128)(2,1)} reshape(bf16[512,2048]{1,0:T(8,128)(2,1)} %reduce.1) | data formatting | bytes 4194304
  204.2 4.8 %all-to-all-start.3 = ((bf16[4,2,131072]{2,1,0:T(2,128)(2,1)}), bf16[4,2,131072]{2,1,0:T(2,128)(2,1)}, u32[]{:S(2)}, u32[]{:S(2)}) async-start(bf16[4,2,131072]{2,1,0:T(2,128)(2,1)} %reshape.245), calls=%async_computation.3 | async-start | bytes 4194304 | tf_op jit(solution)/shard_map/all_to_all | solution.py:120
  211.9 44.8 %all-to-all-done.3 = bf16[4,2,131072]{2,1,0:T(2,128)(2,1)} async-done(((bf16[4,2,131072]{2,1,0:T(2,128)(2,1)}), bf16[4,2,131072]{2,1,0:T(2,128)(2,1)}, u32[]{:S(2)}, u32[]{:S(2)}) %all-to-all-start.3) | async-done | bytes 2097184 | tf_op jit(solution)/shard_map/all_to_all | solution.py:120
  256.8 5.0 %reshape.246 = bf16[512,1,2048]{2,1,0:T(2,128)(2,1)} reshape(bf16[4,2,131072]{2,1,0:T(2,128)(2,1)} %all-to-all-done.3) | data formatting | bytes 4194304
  261.7 4.9 %copy.45 = bf16[1,512,2048]{2,1,0:T(8,128)(2,1)} copy(bf16[1,512,2048]{2,0,1:T(2,128)(2,1)} %bitcast.88) | data formatting | bytes 4194304
  266.6 5.2 %gather_fusion.1 = bf16[256,2048]{1,0:T(8,128)(2,1)} fusion(bf16[512,2048]{1,0:T(8,128)(2,1)} %bitcast.86, s32[1024]{0:T(1024)S(1)} %pad_clamp_fusion), kind=kCustom, calls=%fused_computation.3 | custom fusion | bytes 2098176 | tf_op jit(solution)/shard_map/jit(_take)/gather | solution.py:130
  274.4 4.4 %fusion.23 = bf16[128,2048]{1,0:T(8,128)(2,1)} fusion(bf16[128,2,2048]{2,1,0:T(2,128)(2,1)} %gather.21, pred[128,2]{1,0:T(8,128)(4,1)S(1)} %get-tuple-element.22), kind=kLoop, calls=%fused_computation.39 | loop fusion | flops 786432 | bytes 1573120 | tf_op jit(solution)/shard_map/reduce_sum | solution.py:131
  (65 shorter events, 25.0 us)
Async XLA Ops:
  7.2 141.4 %copy-start = (bf16[1,2048,768]{2,1,0:T(8,128)(2,1)S(1)}, bf16[1,2048,768]{2,1,0:T(8,128)(2,1)}, u32[]{:S(2)}) copy-start(bf16[1,2048,768]{2,1,0:T(8,128)(2,1)} %param.14) | copy-start | bytes 9437188
  16.6 23.1 %all-to-all-start = ((bf16[4,1,128]{2,1,0:T(2,128)(2,1)}), bf16[4,1,128]{2,1,0:T(2,128)(2,1)S(1)}, u32[]{:S(2)}, u32[]{:S(2)}) async-start(bf16[4,1,128]{2,1,0:T(2,128)(2,1)} %copy.36), calls=%async_computation | async-start | bytes 4096 | tf_op jit(solution)/shard_map/all_to_all | solution.py:79
  92.5 51.7 %all-to-all-start.1 = ((bf16[4,128,2048]{2,1,0:T(8,128)(2,1)}), bf16[4,128,2048]{2,1,0:T(8,128)(2,1)}, u32[]{:S(2)}, u32[]{:S(2)}) async-start(bf16[4,128,2048]{2,1,0:T(8,128)(2,1)} %bitcast.89), calls=%async_computation.1 | async-start | bytes 4194304 | tf_op jit(solution)/shard_map/all_to_all | solution.py:78
  96.9 181.9 %reduce-scatter.3.cloned.1.call-start = ((), (), s32[]{:S(2)}) async-start(), calls=%async_computation.7 | async-start | bytes 7077888 | tf_op jit(solution)/shard_map/reduce_scatter | solution.py:99
  144.2 2.5 copy-start.2
  146.7 1.9 copy-start.1
  146.7 2.0 copy-start.7
  151.9 0.9 copy-start.3
  151.9 1.2 copy-start.5
  163.9 40.2 %all-to-all-start.4 = ((bf16[1,4,128]{2,0,1:T(2,128)(2,1)}), bf16[1,4,128]{2,0,1:T(2,128)(2,1)S(1)}, u32[]{:S(2)}, u32[]{:S(2)}) async-start(bf16[1,4,128]{2,0,1:T(2,128)(2,1)} %copy.38), calls=%async_computation.4 | async-start | bytes 4096 | tf_op jit(solution)/shard_map/all_to_all | solution.py:121
  167.2 113.7 %reduce-scatter.5.cloned.1.call-start = ((), (), s32[]{:S(2)}) async-start(), calls=%async_computation.8 | async-start | bytes 3538944 | tf_op jit(solution)/shard_map/reduce_scatter | solution.py:107
  167.4 2.4 copy-start.6
  173.5 4.1 %copy-start.4 = (bf16[512,768]{1,0:T(8,128)(2,1)S(1)}, bf16[512,768]{1,0:T(8,128)(2,1)}, u32[]{:S(2)}) copy-start(bf16[512,768]{1,0:T(8,128)(2,1)} %copy-done.3) | copy-start | bytes 2359300
  204.2 52.6 %all-to-all-start.3 = ((bf16[4,2,131072]{2,1,0:T(2,128)(2,1)}), bf16[4,2,131072]{2,1,0:T(2,128)(2,1)}, u32[]{:S(2)}, u32[]{:S(2)}) async-start(bf16[4,2,131072]{2,1,0:T(2,128)(2,1)} %reshape.245), calls=%async_computation.3 | async-start | bytes 4194304 | tf_op jit(solution)/shard_map/all_to_all | solution.py:120
Sparse Core Ops, SparseCore 0:
  158.8 60.8 reduce-scatter.2
  223.6 46.0 reduce-scatter.4
where the time goes:
time: 289 us; the launch traced here: 288 us
  waiting for transfers between devices  86.4 us (30%)
  local copies, waits for them, and re-layouts  55.8 us (19%)
  blocking collectives  52.8 us (18%)
  matrix products  30.2 us (10%)
  other arithmetic  28.8 us (10%)
  starting transfers between devices  19.3 us (7%)
  between operations  14.3 us (5%)
    all_to_all x1, blocking collectives, shards(): lax.all_to_all(rows_x, 'expert', split_axis=0, concat_axis=1, tiled=True)  52.8 us
    all_to_all x1, waiting for transfers between devices, shards(): lax.all_to_all(jnp.stack(row_list), 'expert', split_axis=1, concat_axis=0...  44.8 us
    all_to_all x1, waiting for transfers between devices, shards(): lax.all_to_all(rows_dy, 'expert', split_axis=0, concat_axis=1, tiled=True)  41.5 us
    unnamed x23, local copies, waits for them, and re-layouts  19 us
    unnamed x2, other arithmetic  14.5 us
    gather x2, local copies, waits for them, and re-layouts, shards(): picked = jnp.take(flat_rows, dest, axis=0).reshape(tok_rows, top, feature)  7.81 us
    gather x1, local copies, waits for them, and re-layouts, gather_rows(): jnp.take(cotangent, source, axis=0)  6.36 us
    all_to_all x1, starting transfers between devices, shards(): lax.all_to_all(rows_c.astype(jnp.bfloat16), 'expert', split_axis=0, conca...  6.35 us
  transfers between devices with their start and end apart: 6, of which 2 were waited for; matrix products, arithmetic and copies ran while one was open for 32% of the time, Pallas kernels for 0%

commit v1 on v0

--- a/solution.py
+++ b/solution.py
@@ -2,6 +2,29 @@
 import jax.numpy as jnp
 from jax import lax
 from jax.sharding import PartitionSpec as P
+
+
+def cut_along(x, dim, count):
+    lengths = x.shape
+    parts = x.reshape(*lengths[:dim], count, lengths[dim] // count, *lengths[dim + 1 :])
+    return jnp.moveaxis(parts, dim, 0)
+
+
+def laid_out(pieces, dim):
+    pieces = jnp.moveaxis(pieces, 0, dim)
+    shape = pieces.shape
+    return pieces.reshape(*shape[:dim], shape[dim] * shape[dim + 1], *shape[dim + 2 :])
+
+
+def swapped_with_each(value, axis, split_dim, concat_dim):
+    size, position = (lax.axis_size(axis), lax.axis_index(axis))
+    blocks = cut_along(value, split_dim, size)
+    done = [blocks[position]]
+    for step in range(1, size):
+        sent = blocks[position ^ step]
+        done.append(lax.ppermute(sent, axis, [(i, i ^ step) for i in range(size)]))
+    blocks = jnp.stack(done)[position ^ jnp.arange(size)]
+    return laid_out(blocks, concat_dim)
 
 
 def slot_table(expert_ids, experts_all, capacity):
@@ -74,7 +97,7 @@
     rows_dy = rows_dy.reshape(experts_all, capacity, feature)
     rows_c = rows_c.reshape(experts_all, capacity)
     recv_x, recv_dy, recv_c = (
-        lax.all_to_all(rows_x, "expert", split_axis=0, concat_axis=1, tiled=True),
+        swapped_with_each(rows_x, "expert", 0, 1),
         lax.all_to_all(rows_dy, "expert", split_axis=0, concat_axis=1, tiled=True),
         lax.all_to_all(
             rows_c.astype(jnp.bfloat16), "expert", split_axis=0, concat_axis=1, tiled=True

time: 289 us -> 292 us (1.010)
  blocking collectives: 52.8 us -> 0 us
  waiting for transfers between devices: 86.4 us -> 131 us
  local copies, waits for them, and re-layouts: 55.8 us -> 61.1 us
  starting transfers between devices: 19.3 us -> 24.3 us
    ppermute x0 -> x3, waiting for transfers between devices: none -> 86.3 us  [swapped_with_each(): done.append(lax.ppermute(sent, axis, [(i, i ^ step) for i in range(size)]))]
    all_to_all x1 -> x0, blocking collectives: 52.8 us -> none  [shards(): lax.all_to_all(rows_x, 'expert', split_axis=0, concat_axis=1, tiled=True)]
    all_to_all x1, waiting for transfers between devices: 41.5 us -> 0.01 us  [shards(): lax.all_to_all(rows_dy, 'expert', split_axis=0, concat_axis=1, tiled=True)]
    ppermute x0 -> x3, starting transfers between devices: none -> 4.53 us  [swapped_with_each(): done.append(lax.ppermute(sent, axis, [(i, i ^ step) for i in range(size)]))]
    gather x0 -> x1, local copies, waits for them, and re-layouts: none -> 3.58 us  [swapped_with_each(): blocks = jnp.stack(done)[position ^ jnp.arange(size)]]
  transfers between devices with their start and end apart: 6 -> 9, of which waited for: 2 -> 3; matrix products, arithmetic and copies ran while one was open for 32% -> 34% of each run, Pallas kernels for 0% -> 0%
where the time goes in v1:
time: 292 us; the launch traced here: 291 us
  waiting for transfers between devices  131 us (45%)
  local copies, waits for them, and re-layouts  61.1 us (21%)
  other arithmetic  30.3 us (10%)
  matrix products  30.2 us (10%)
  starting transfers between devices  24.3 us (8%)
  between operations  14.3 us (5%)
    ppermute x3, waiting for transfers between devices, swapped_with_each(): done.append(lax.ppermute(sent, axis, [(i, i ^ step) for i in range(size)]))  86.3 us
    all_to_all x1, waiting for transfers between devices, shards(): lax.all_to_all(jnp.stack(row_list), 'expert', split_axis=1, concat_axis=0...  44.8 us
    unnamed x23, local copies, waits for them, and re-layouts  19 us
    unnamed x2, other arithmetic  14.5 us
    gather x2, local copies, waits for them, and re-layouts, shards(): picked = jnp.take(flat_rows, dest, axis=0).reshape(tok_rows, top, feature)  7.81 us
    gather x1, local copies, waits for them, and re-layouts, gather_rows(): jnp.take(tokens, source, axis=0)  6.4 us
    gather x1, local copies, waits for them, and re-layouts, gather_rows(): jnp.take(cotangent, source, axis=0)  6.35 us
    all_to_all x1, starting transfers between devices, shards(): lax.all_to_all(rows_c.astype(jnp.bfloat16), 'expert', split_axis=0, conca...  6.35 us
  transfers between devices with their start and end apart: 9, of which 3 were waited for; matrix products, arithmetic and copies ran while one was open for 34% of the time, Pallas kernels for 0%

profile of v1, /device:TPU:0, one launch (start us, length us, event | category | flops | bytes accessed | tf_op | source)
XLA Modules:
  0.0 291.5 jit_solution(647359564526285780)
XLA Ops:
  12.6 3.4 %gather_fusion = bf16[512]{0:T(512)(128)(2,1)S(1)} fusion(bf16[256]{0:T(256)(128)(2,1)S(1)} %reshape.189, s32[1024]{0:T(1024)S(1)} %pad_clamp_fusion.3), kind=kCustom, calls=%fused_computation.2 | custom fusion | bytes 4096 | tf_op jit(solution)/shard_map/jit(_take)/gather | solution.py:54
  16.6 6.3 %all-to-all-start = ((bf16[4,1,128]{2,1,0:T(2,128)(2,1)}), bf16[4,1,128]{2,1,0:T(2,128)(2,1)S(1)}, u32[]{:S(2)}, u32[]{:S(2)}) async-start(bf16[4,1,128]{2,1,0:T(2,128)(2,1)} %copy.36), calls=%async_computation | async-start | bytes 4096 | tf_op jit(solution)/shard_map/all_to_all | solution.py:102
  23.0 6.4 %gather_fusion.5 = bf16[512,2048]{1,0:T(8,128)(2,1)} fusion(bf16[128,2048]{1,0:T(8,128)(2,1)} %param.9, s32[1024]{0:T(1024)S(1)} %pad_clamp_fusion.2), kind=kCustom, calls=%fused_computation.1.clone | custom fusion | bytes 4196352 | tf_op jit(solution)/shard_map/jit(_take)/gather | solution.py:49
  29.4 6.4 %gather_fusion.4 = bf16[512,2048]{1,0:T(8,128)(2,1)} fusion(bf16[128,2048]{1,0:T(8,128)(2,1)} %param.10, s32[1024]{0:T(1024)S(1)} %pad_clamp_fusion.2), kind=kCustom, calls=%fused_computation.clone | custom fusion | bytes 4196352 | tf_op jit(solution)/shard_map/jit(_take)/gather | solution.py:51
  35.7 3.9 %select_select_fusion.1 = (bf16[512,2048]{1,0:T(8,128)(2,1)}, bf16[512,2048]{1,0:T(8,128)(2,1)}) fusion(bf16[512,2048]{1,0:T(8,128)(2,1)} %gather_fusion.4, pred[512]{0:T(512)(128)(4,1)S(1)} %get-tuple-element.25, pred[512]{0:T(512)(128)(4,1)S(1)} %get-tuple-element.24, bf16[512,2048]{1,0:T(8,128)(2,1)} %gather_fusion.5), kind=kLoop, calls=%fused_computation.31 | loop fusion | flops 4194304 | bytes 8389632 | tf_op jit(solution)/shard_map/jit(_where)/select_n | solution.py:50
  39.6 5.1 %all-to-all-start.1 = ((bf16[4,128,2048]{2,1,0:T(8,128)(2,1)}), bf16[4,128,2048]{2,1,0:T(8,128)(2,1)}, u32[]{:S(2)}, u32[]{:S(2)}) async-start(bf16[4,128,2048]{2,1,0:T(8,128)(2,1)} %bitcast.102), calls=%async_computation.1 | async-start | bytes 4194304 | tf_op jit(solution)/shard_map/all_to_all | solution.py:101
  46.4 3.9 %collective-permute-start.2 = (bf16[1,128,2048]{2,1,0:T(8,128)(2,1)S(1)}, bf16[1,128,2048]{2,1,0:T(8,128)(2,1)S(1)}, u32[]{:S(2)}, u32[]{:S(2)}) collective-permute-start(bf16[1,128,2048]{2,1,0:T(8,128)(2,1)S(1)} %get-tuple-element.31), channel_id=1, source_target_pairs={{0,3},{1,2},{2,1},{3,0},{4,7},{5,6},{6,5},{7,4},{8,11},{9,10},{10,... | collective-permute-start | bytes 1572872 | tf_op jit(solution)/shard_map/ppermute | solution.py:25
  50.9 44.4 %collective-permute-done.2 = bf16[1,128,2048]{2,1,0:T(8,128)(2,1)S(1)} collective-permute-done((bf16[1,128,2048]{2,1,0:T(8,128)(2,1)S(1)}, bf16[1,128,2048]{2,1,0:T(8,128)(2,1)S(1)}, u32[]{:S(2)}, u32[]{:S(2)}) %collective-permute-start.2) | collective-permute-done | bytes 524320 | tf_op jit(solution)/shard_map/ppermute | solution.py:25
  95.3 42.0 %collective-permute-done.1 = bf16[1,128,2048]{2,1,0:T(8,128)(2,1)S(1)} collective-permute-done((bf16[1,128,2048]{2,1,0:T(8,128)(2,1)S(1)}, bf16[1,128,2048]{2,1,0:T(8,128)(2,1)S(1)}, u32[]{:S(2)}, u32[]{:S(2)}) %collective-permute-start.1) | collective-permute-done | bytes 524320 | tf_op jit(solution)/shard_map/ppermute | solution.py:25
  138.9 3.6 %gather_fusion.1 = bf16[4,128,2048]{2,1,0:T(8,128)(2,1)} fusion(bf16[4,128,2048]{2,1,0:T(8,128)(2,1)} %maximum_bitcast_fusion, s32[1024]{0:T(1024)S(1)} %pad_clamp_fusion.1), kind=kCustom, calls=%fused_computation.3 | custom fusion | bytes 4194320 | tf_op jit(solution)/shard_map/gather | solution.py:26
  142.5 5.5 %fusion.5 = f32[512,768]{1,0:T(8,128)} fusion(bf16[512,2048]{1,0:T(8,128)(2,1)} %bitcast.104, bf16[1,2048,768]{2,1,0:T(8,128)(2,1)} %param.13), kind=kOutput, calls=%fused_computation.18 | convolution fusion | flops 1610612736 | bytes 6815744 | tf_op jit(solution)/shard_map/dot_general | solution.py:60
  156.8 5.6 %convolution_convert_fusion = bf16[2048,1536]{1,0:T(8,128)(2,1)} fusion(bf16[512,2048]{1,0:T(8,128)(2,1)S(1)} %bitcast.106, bf16[512,768]{1,0:T(8,128)(2,1)S(1)} %get-tuple-element.29, bf16[512,768]{1,0:T(8,128)(2,1)S(1)} %get-tuple-element.28), kind=kOutput, calls=%fused_computation.7 | convolution fusion | flops 3227516928 | bytes 9961472 | tf_op jit(solution)/shard_map/dot_general | solution.py:117
  162.4 4.7 %fusion.1 = bf16[512]{0:T(512)(128)(2,1)S(1)} fusion(bf16[4,128,2048]{2,1,0:T(8,128)(2,1)} %all-to-all-done.1, bf16[512,768]{1,0:T(8,128)(2,1)} %get-tuple-element.27, bf16[1,768,2048]{2,1,0:T(8,128)(2,1)} %param.15), kind=kOutput, calls=%fused_computation.12 | convolution fusion | flops 1613757952 | bytes 6030336 | tf_op jit(solution)/shard_map/dot_general | solution.py:65
  173.6 3.6 %convolution_convert_fusion.1 = bf16[768,2048]{1,0:T(8,128)(2,1)} fusion(bf16[512,768]{1,0:T(8,128)(2,1)S(1)} %copy-done.6, bf16[512,2048]{1,0:T(8,128)(2,1)S(1)} %fusion.2), kind=kOutput, calls=%fused_computation.15 | convolution fusion | flops 1612185600 | bytes 6029312 | tf_op jit(solution)/shard_map/dot_general | solution.py:120
  177.2 4.1 %fusion.3 = f32[512,2048]{1,0:T(8,128)S(1)} fusion(bf16[512,768]{1,0:T(8,128)(2,1)} %copy-done.5, bf16[1,2048,768]{2,1,0:T(8,128)(2,1)} %param.13), kind=kOutput, calls=%fused_computation.16 | convolution fusion | flops 1610612736 | bytes 8126464 | tf_op jit(solution)/shard_map/dot_general | solution.py:77
  183.1 5.3 %copy.46 = bf16[1,512,2048]{2,0,1:T(2,128)(2,1)} copy(bf16[1,512,2048]{2,1,0:T(8,128)(2,1)S(1)} %fusion.16) | data formatting | bytes 4194304 | tf_op jit(solution)/shard_map/stack | solution.py:143
  188.9 14.5 %reduce.1 = bf16[512,2048]{1,0:T(8,128)(2,1)} reduce(bf16[512,1,2048]{2,1,0:T(2,128)(2,1)} %bitcast.100, bf16[]{:T(256)} %broadcast.174), dimensions={1}, to_apply=%bitcast.96.reduce_sub_computation | reduce | bytes 4194306
  203.4 4.6 %reshape.264 = bf16[4,2,131072]{2,1,0:T(2,128)(2,1)} reshape(bf16[512,2048]{1,0:T(8,128)(2,1)} %reduce.1) | data formatting | bytes 4194304
  208.0 4.8 %all-to-all-start.2 = ((bf16[4,2,131072]{2,1,0:T(2,128)(2,1)}), bf16[4,2,131072]{2,1,0:T(2,128)(2,1)}, u32[]{:S(2)}, u32[]{:S(2)}) async-start(bf16[4,2,131072]{2,1,0:T(2,128)(2,1)} %reshape.264), calls=%async_computation.2 | async-start | bytes 4194304 | tf_op jit(solution)/shard_map/all_to_all | solution.py:143
  215.7 44.8 %all-to-all-done.2 = bf16[4,2,131072]{2,1,0:T(2,128)(2,1)} async-done(((bf16[4,2,131072]{2,1,0:T(2,128)(2,1)}), bf16[4,2,131072]{2,1,0:T(2,128)(2,1)}, u32[]{:S(2)}, u32[]{:S(2)}) %all-to-all-start.2) | async-done | bytes 2097184 | tf_op jit(solution)/shard_map/all_to_all | solution.py:143
  260.5 5.0 %reshape.265 = bf16[512,1,2048]{2,1,0:T(2,128)(2,1)} reshape(bf16[4,2,131072]{2,1,0:T(2,128)(2,1)} %all-to-all-done.2) | data formatting | bytes 4194304
  265.5 4.9 %copy.45 = bf16[1,512,2048]{2,1,0:T(8,128)(2,1)} copy(bf16[1,512,2048]{2,0,1:T(2,128)(2,1)} %bitcast.101) | data formatting | bytes 4194304
  270.4 5.2 %gather_fusion.2 = bf16[256,2048]{1,0:T(8,128)(2,1)} fusion(bf16[512,2048]{1,0:T(8,128)(2,1)} %bitcast.99, s32[1024]{0:T(1024)S(1)} %pad_clamp_fusion), kind=kCustom, calls=%fused_computation.4 | custom fusion | bytes 2098176 | tf_op jit(solution)/shard_map/jit(_take)/gather | solution.py:153
  278.2 4.4 %fusion.23 = bf16[128,2048]{1,0:T(8,128)(2,1)} fusion(bf16[128,2,2048]{2,1,0:T(2,128)(2,1)} %gather.25, pred[128,2]{1,0:T(8,128)(4,1)S(1)} %get-tuple-element.22), kind=kLoop, calls=%fused_computation.41 | loop fusion | flops 786432 | bytes 1573120 | tf_op jit(solution)/shard_map/reduce_sum | solution.py:154
  (75 shorter events, 35.1 us)
Async XLA Ops:
  7.2 145.1 %copy-start = (bf16[1,2048,768]{2,1,0:T(8,128)(2,1)S(1)}, bf16[1,2048,768]{2,1,0:T(8,128)(2,1)}, u32[]{:S(2)}) copy-start(bf16[1,2048,768]{2,1,0:T(8,128)(2,1)} %param.14) | copy-start | bytes 9437188
  16.6 23.0 %all-to-all-start = ((bf16[4,1,128]{2,1,0:T(2,128)(2,1)}), bf16[4,1,128]{2,1,0:T(2,128)(2,1)S(1)}, u32[]{:S(2)}, u32[]{:S(2)}) async-start(bf16[4,1,128]{2,1,0:T(2,128)(2,1)} %copy.36), calls=%async_computation | async-start | bytes 4096 | tf_op jit(solution)/shard_map/all_to_all | solution.py:102
  39.6 108.3 %all-to-all-start.1 = ((bf16[4,128,2048]{2,1,0:T(8,128)(2,1)}), bf16[4,128,2048]{2,1,0:T(8,128)(2,1)}, u32[]{:S(2)}, u32[]{:S(2)}) async-start(bf16[4,128,2048]{2,1,0:T(8,128)(2,1)} %bitcast.102), calls=%async_computation.1 | async-start | bytes 4194304 | tf_op jit(solution)/shard_map/all_to_all | solution.py:101
  44.7 237.9 %reduce-scatter.3.cloned.1.call-start = ((), (), s32[]{:S(2)}) async-start(), calls=%async_computation.6 | async-start | bytes 7077888 | tf_op jit(solution)/shard_map/reduce_scatter | solution.py:122
  46.4 48.9 %collective-permute-start.2 = (bf16[1,128,2048]{2,1,0:T(8,128)(2,1)S(1)}, bf16[1,128,2048]{2,1,0:T(8,128)(2,1)S(1)}, u32[]{:S(2)}, u32[]{:S(2)}) collective-permute-start(bf16[1,128,2048]{2,1,0:T(8,128)(2,1)S(1)} %get-tuple-element.31), channel_id=1, source_target_pairs={{0,3},{1,2},{2,1},{3,0},{4,7},{5,6},{6,5},{7,4},{8,11},{9,10},{10,... | collective-permute-start | bytes 1572872 | tf_op jit(solution)/shard_map/ppermute | solution.py:25
  50.3 87.0 %collective-permute-start.1 = (bf16[1,128,2048]{2,1,0:T(8,128)(2,1)S(1)}, bf16[1,128,2048]{2,1,0:T(8,128)(2,1)S(1)}, u32[]{:S(2)}, u32[]{:S(2)}) collective-permute-start(bf16[1,128,2048]{2,1,0:T(8,128)(2,1)S(1)} %get-tuple-element.32), channel_id=1, source_target_pairs={{0,2},{1,3},{2,0},{3,1},{4,6},{5,7},{6,4},{7,5},{8,10},{9,11},{10,... | collective-permute-start | bytes 1572872 | tf_op jit(solution)/shard_map/ppermute | solution.py:25
  50.3 87.0 %collective-permute-start = (bf16[1,128,2048]{2,1,0:T(8,128)(2,1)S(1)}, bf16[1,128,2048]{2,1,0:T(8,128)(2,1)S(1)}, u32[]{:S(2)}, u32[]{:S(2)}) collective-permute-start(bf16[1,128,2048]{2,1,0:T(8,128)(2,1)S(1)} %get-tuple-element.33), channel_id=1, source_target_pairs={{0,1},{1,0},{2,3},{3,2},{4,5},{5,4},{6,7},{7,6},{8,9},{9,8},{10,11... | collective-permute-start | bytes 1572872 | tf_op jit(solution)/shard_map/ppermute | solution.py:25
  147.9 2.5 copy-start.2
  150.5 1.9 copy-start.1
  150.5 2.0 copy-start.7
  155.6 0.9 copy-start.3
  155.6 1.2 copy-start.5
  167.7 40.3 %all-to-all-start.3 = ((bf16[1,4,128]{2,0,1:T(2,128)(2,1)}), bf16[1,4,128]{2,0,1:T(2,128)(2,1)S(1)}, u32[]{:S(2)}, u32[]{:S(2)}) async-start(bf16[1,4,128]{2,0,1:T(2,128)(2,1)} %copy.38), calls=%async_computation.3 | async-start | bytes 4096 | tf_op jit(solution)/shard_map/all_to_all | solution.py:144
  170.9 113.7 %reduce-scatter.5.cloned.1.call-start = ((), (), s32[]{:S(2)}) async-start(), calls=%async_computation.7 | async-start | bytes 3538944 | tf_op jit(solution)/shard_map/reduce_scatter | solution.py:130
  171.2 2.4 copy-start.6
  177.2 4.1 %copy-start.4 = (bf16[512,768]{1,0:T(8,128)(2,1)S(1)}, bf16[512,768]{1,0:T(8,128)(2,1)}, u32[]{:S(2)}) copy-start(bf16[512,768]{1,0:T(8,128)(2,1)} %copy-done.3) | copy-start | bytes 2359300
  208.0 52.6 %all-to-all-start.2 = ((bf16[4,2,131072]{2,1,0:T(2,128)(2,1)}), bf16[4,2,131072]{2,1,0:T(2,128)(2,1)}, u32[]{:S(2)}, u32[]{:S(2)}) async-start(bf16[4,2,131072]{2,1,0:T(2,128)(2,1)} %reshape.264), calls=%async_computation.2 | async-start | bytes 4194304 | tf_op jit(solution)/shard_map/all_to_all | solution.py:143
Sparse Core Ops, SparseCore 0:
  162.5 60.8 reduce-scatter.2
  227.4 46.0 reduce-scatter.4
